TPU v7x, 256 devices: a whole 4x4x8 slice. The times are simulated.
256 devices in a mesh: dp: 64 (over x, z, core), cent: 4 (over y).
Axes of the slice: x: 4, y: 4, z: 8, core: 2. Of those that a mesh axis runs over, the one named last changes fastest.
Arguments:
- documents: bfloat16 [131072, 2048], P(('dp', 'cent')), may hold values from -6 to 6
- assigned: int32 [131072], P(('dp', 'cent')), may hold values from 0 to 98303, as said below
- centroids: bfloat16 [98304, 2048], P(('dp', 'cent')), may hold values from -6 to 6
- owner_slot: int32 [98304], replicated, may hold values from 0 to 98303, as said below
Outputs:
- prototypicality: float32 [131072], P(('dp', 'cent'))
- redundancy: float32 [131072], P(('dp', 'cent'))
- cluster_stats: float32 [3, 98304], P(None, ('dp', 'cent'))
Inputs may be any that keep to these rules, and one draw needn't show every extreme that they name: `owner_slot`: A permutation of the cluster numbers. `assigned`: of the 512 documents of one device, at most 4 have a slot in any one owner's block of 384 slots, and at most 10 have slots with the owners that share one dp index; in every draw some device reaches 10, and one owner receives exactly 4 from every device.
All inputs are finite; a program needn't handle non-finite values.
Results may differ from a plain program's by a relative error of at most 0.0003.
Values may be sent and summed in bfloat16 or wider, within the bound.
A program may use at most 64 MiB of HBM per device.

v0:
```python
import math

import jax
import jax.numpy as jnp
from jax import lax
from jax.sharding import Mesh
from jax.sharding import PartitionSpec as P

DP = ("dp_0", "dp_1", "dp_2")
DP_CENT = ("dp_0", "dp_1", "dp_2", "cent")


def split_up(value, dim, peers):
    lengths = value.shape
    blocks = value.reshape(*lengths[:dim], peers, lengths[dim] // peers, *lengths[dim + 1 :])
    return jnp.moveaxis(blocks, dim, 0)


def laid_out(blocks, dim):
    blocks = jnp.moveaxis(blocks, 0, dim)
    lengths = blocks.shape
    return blocks.reshape(*lengths[:dim], lengths[dim] * lengths[dim + 1], *lengths[dim + 2 :])


def moved_by_axis(blocks, axes, order):
    lengths = [lax.axis_size(a) for a in axes]
    blocks = blocks.reshape(*lengths, *blocks.shape[1:])
    for k in order:
        blocks = lax.all_to_all(blocks, axes[k], split_axis=k, concat_axis=k, tiled=True)
    return blocks.reshape(-1, *blocks.shape[len(axes) :])


def exchange_by_chip(value, groups, order, split_dim, concat_dim):
    peers = lax.axis_size(groups[0]) * lax.axis_size(groups[1])
    blocks = split_up(value, split_dim, peers)
    return laid_out(moved_by_axis(blocks, groups, order), concat_dim)


def sent_together(arrays, axis, split_dim, concat_dim, along):
    ends, at = ([], 0)
    for a in arrays[:-1]:
        at += a.shape[along]
        ends.append(at)
    both = jnp.concatenate(arrays, axis=along)
    return tuple(
        jnp.split(
            lax.all_to_all(both, axis, split_axis=split_dim, concat_axis=concat_dim, tiled=True),
            ends,
            axis=along,
        )
    )


def bucket_positions(target, groups, capacity):
    length = target.shape[0]
    indicator = (target[:, None] == jnp.arange(groups, dtype=jnp.int32)[None, :]).astype(
        jnp.bfloat16
    )
    earlier = (
        lax.broadcasted_iota(jnp.int32, (length, length), 0)
        > lax.broadcasted_iota(jnp.int32, (length, length), 1)
    ).astype(jnp.bfloat16)
    before = jnp.dot(earlier, indicator, preferred_element_type=jnp.float32)
    rank_ids = jnp.sum(before * indicator.astype(jnp.float32), axis=1).astype(jnp.int32)
    return jnp.where(target < groups, target * capacity + rank_ids, groups * capacity)


def owner_work(incoming, incoming_tags, centroids):
    table_rows = centroids.shape[0]
    width = incoming.shape[1]
    length = incoming_tags.shape[0]
    is_live = incoming_tags >= 0
    safe_slot = jnp.clip(incoming_tags, 0, table_rows - 1)
    cent_sq = jnp.einsum("kd,kd->k", centroids, centroids, preferred_element_type=jnp.float32)
    cent_vec = centroids[safe_slot]
    cross_dot = jnp.einsum("sd,sd->s", incoming, cent_vec, preferred_element_type=jnp.float32)
    self_sq = jnp.einsum("sd,sd->s", incoming, incoming, preferred_element_type=jnp.float32)
    inverse_norm = lax.rsqrt(self_sq + 1.0)
    similarity = cross_dot * inverse_norm * lax.rsqrt(cent_sq[safe_slot] + 1.0)
    members = (incoming_tags[:, None] == jnp.arange(table_rows, dtype=jnp.int32)[None, :]).astype(
        jnp.float32
    )
    live_weight = is_live.astype(jnp.float32)
    moments = jnp.stack(
        [live_weight, live_weight * similarity, live_weight * similarity * similarity]
    )
    cluster_totals = jnp.dot(
        moments, members, precision=lax.Precision.HIGHEST, preferred_element_type=jnp.float32
    )
    count_floor = jnp.maximum(cluster_totals[0], 1.0)
    mean_sim = cluster_totals[1] / count_floor
    variance = jnp.maximum(cluster_totals[2] / count_floor - mean_sim * mean_sim, 0.0)
    proto_score = jnp.where(
        is_live,
        (mean_sim[safe_slot] - similarity) / jnp.sqrt(variance[safe_slot] + 1.0 / width),
        0.0,
    )
    gram_block = lax.dot_general(
        incoming, incoming, (((1,), (1,)), ((), ())), preferred_element_type=jnp.float32
    )
    cosine = gram_block * inverse_norm[:, None] * inverse_norm[None, :]
    not_self = lax.broadcasted_iota(jnp.int32, (length, length), 0) != lax.broadcasted_iota(
        jnp.int32, (length, length), 1
    )
    same_cluster = (incoming_tags[:, None] == incoming_tags[None, :]) & is_live[:, None] & not_self
    redundant = math.sqrt(width) * jnp.max(jnp.where(same_cluster, cosine, 0.0), axis=1)
    return (cluster_totals, proto_score, redundant)


def local(documents, assigned, centroids, owner_slot):
    doc_count, width = documents.shape
    table_rows = centroids.shape[0]
    dp_count = lax.axis_size(DP)
    cent_count = lax.axis_size("cent")
    owner_count = dp_count * cent_count
    pair_cap = 2 * doc_count // owner_count
    row_cap = 5 * cent_count * pair_cap // 8
    slot_ids = owner_slot[assigned]
    owner_ids = slot_ids // table_rows
    local_ids = slot_ids % table_rows
    row_ids = owner_ids // cent_count
    col_ids = owner_ids % cent_count
    first_pos = bucket_positions(row_ids, dp_count, row_cap)
    outgoing = jnp.zeros((dp_count * row_cap, width), jnp.bfloat16).at[first_pos].set(documents)
    tag_ids = (
        jnp.full((dp_count * row_cap,), -1, jnp.int32)
        .at[first_pos]
        .set(col_ids * table_rows + local_ids)
    )
    relayed, relayed_tags = (
        exchange_by_chip(
            outgoing.reshape(dp_count, row_cap, width), (("dp_0", "dp_1"), "dp_2"), (1, 0), 0, 0
        ),
        exchange_by_chip(
            tag_ids.reshape(dp_count, row_cap), (("dp_0", "dp_1"), "dp_2"), (1, 0), 0, 0
        ),
    )
    relayed = relayed.reshape(-1, width)
    relayed_tags = relayed_tags.reshape(-1)
    relay_live = relayed_tags >= 0
    relay_target = jnp.where(relay_live, relayed_tags // table_rows, cent_count)
    inner_cap = dp_count * pair_cap
    second_pos = bucket_positions(relay_target, cent_count, inner_cap)
    forward = (
        jnp.zeros((cent_count * inner_cap, width), jnp.bfloat16)
        .at[second_pos]
        .set(relayed, mode="drop")
    )
    forward_tags = (
        jnp.full((cent_count * inner_cap,), -1, jnp.int32)
        .at[second_pos]
        .set(jnp.where(relay_live, relayed_tags % table_rows, -1), mode="drop")
    )
    incoming, incoming_tags = (
        lax.all_to_all(
            forward.reshape(cent_count, inner_cap, width),
            "cent",
            split_axis=0,
            concat_axis=0,
            tiled=True,
        ),
        lax.all_to_all(
            forward_tags.reshape(cent_count, inner_cap),
            "cent",
            split_axis=0,
            concat_axis=0,
            tiled=True,
        ),
    )
    cluster_totals, proto_score, redundant = owner_work(
        incoming.reshape(-1, width), incoming_tags.reshape(-1), centroids
    )
    back_score, back_redundant = sent_together(
        (proto_score.reshape(cent_count, inner_cap), redundant.reshape(cent_count, inner_cap)),
        "cent",
        0,
        0,
        1,
    )
    safe_pos = jnp.clip(second_pos, 0, cent_count * inner_cap - 1)
    relay_score = jnp.where(relay_live, back_score.reshape(-1)[safe_pos], 0.0)
    relay_redundant = jnp.where(relay_live, back_redundant.reshape(-1)[safe_pos], 0.0)
    home_score, home_redundant = sent_together(
        (relay_score.reshape(dp_count, row_cap), relay_redundant.reshape(dp_count, row_cap)),
        DP,
        0,
        0,
        1,
    )
    prototypicality = home_score.reshape(-1)[first_pos]
    redundancy = home_redundant.reshape(-1)[first_pos]
    return (prototypicality, redundancy, cluster_totals)


def solution(mesh):
    split = Mesh(
        mesh.devices.reshape(4, 8, 2, mesh.shape["cent"]), ("dp_0", "dp_1", "dp_2", "cent")
    )
    placed = (P(DP_CENT, None), P(DP_CENT), P(DP_CENT, None), P())
    return jax.shard_map(
        local,
        mesh=split,
        in_specs=placed,
        out_specs=(P(DP_CENT), P(DP_CENT), P(None, DP_CENT)),
        check_vma=False,
    )
```

profile of v0, /device:TPU:1, one launch (start us, length us, event | category | flops | bytes accessed | tf_op | source)
XLA Modules:
  0.0 263.2 jit_solution(11740768306604892653)
XLA Ops:
  0.6 0.7 compare_select_fusion.6
  1.4 0.3 copy-done
  1.6 3.1 %gather_fusion = s32[512]{0:T(512)S(1)} fusion(s32[98304]{0:T(1024)S(1)} %copy-done, s32[1024]{0:T(1024)S(1)} %pad_clamp_fusion.2), kind=kCustom, calls=%fused_computation | custom fusion | bytes 6144 | tf_op jit(solution)/shard_map/gather | solution.py:118
  4.8 0.3 fusion.10
  5.2 2.4 scatter_custom_fusion
  7.9 0.5 broadcast.527
  8.4 0.7 reduce.14
  9.1 0.7 reshape.498
  9.7 6.4 %all-to-all-start = ((s32[2,1,320]{2,1,0:T(1,128)}), s32[2,1,320]{2,1,0:T(1,128)S(1)}, u32[]{:S(2)}, u32[]{:S(2)}) async-start(s32[2,1,320]{2,1,0:T(1,128)} %reshape.498), calls=%async_computation | async-start | bytes 6144 | tf_op jit(solution)/shard_map/all_to_all | solution.py:29
  16.1 5.4 %scatter_custom_fusion.2 = bf16[640,2048]{1,0:T(8,128)(2,1)S(1)} fusion(s32[512]{0:T(512)S(1)} %bitcast.62, bf16[512,2048]{1,0:T(8,128)(2,1)} %param.4, bf16[]{:T(256)} %constant.88.clone.1), kind=kCustom, calls=%fused_computation.28 | custom fusion | bytes 2621952 | tf_op jit(solution)/shard_map/scatter | solution.py:124
  21.6 2.8 %reshape_reshape_reshape.11 = bf16[32,2,1,10,2048]{4,3,1,0,2:T(8,128)(2,1)} reshape(bf16[640,2048]{1,0:T(8,128)(2,1)S(1)} %scatter_custom_fusion.2) | data formatting | bytes 5242880 | tf_op jit(solution)/shard_map/reshape;reshape;reshape | solution.py:27
  24.4 5.2 %copy.17 = bf16[32,2,1,10,2048]{4,0,3,2,1:T(8,128)(2,1)} copy(bf16[32,2,1,10,2048]{4,3,1,0,2:T(8,128)(2,1)} %reshape_reshape_reshape.11) | data formatting | bytes 5242880 | tf_op jit(solution)/shard_map/reshape;reshape;reshape | solution.py:27
  29.5 3.9 %all-to-all-start.3 = ((bf16[32,2,1,10,2048]{4,0,3,2,1:T(8,128)(2,1)}), bf16[32,2,1,10,2048]{4,0,3,2,1:T(8,128)(2,1)S(1)}, u32[]{:S(2)}, u32[]{:S(2)}) async-start(bf16[32,2,1,10,2048]{4,0,3,2,1:T(8,128)(2,1)} %copy.17), calls=%async_computation.3 | async-start | bytes 5242880 | tf_op jit(solution)/shard_map/all_to_all | solution.py:29
  33.4 0.7 reduce.15
  34.2 0.7 copy.16
  34.9 1.4 all-to-all-done.3
  36.3 9.3 %all-to-all-start.1 = ((s32[32,2,1,10]{3,1,2,0:T(2,128)}), s32[32,2,1,10]{3,1,2,0:T(2,128)S(1)}, u32[]{:S(2)}, u32[]{:S(2)}) async-start(s32[32,2,1,10]{3,1,2,0:T(2,128)} %copy.16), calls=%async_computation.1 | async-start | bytes 65536 | tf_op jit(solution)/shard_map/all_to_all | solution.py:29
  45.6 4.2 %copy.18 = bf16[32,2,1,10,2048]{4,1,3,2,0:T(2,128)(2,1)} copy(bf16[32,2,1,10,2048]{4,0,3,2,1:T(8,128)(2,1)S(1)} %all-to-all-done.3) | data formatting | bytes 5242880 | tf_op jit(solution)/shard_map/all_to_all | solution.py:29
  49.8 4.6 %all-to-all-done.1 = s32[32,2,1,10]{3,1,2,0:T(2,128)S(1)} async-done(((s32[32,2,1,10]{3,1,2,0:T(2,128)}), s32[32,2,1,10]{3,1,2,0:T(2,128)S(1)}, u32[]{:S(2)}, u32[]{:S(2)}) %all-to-all-start.1) | async-done | bytes 2592 | tf_op jit(solution)/shard_map/all_to_all | solution.py:29
  54.4 4.7 %all-to-all-start.4 = ((bf16[32,2,1,10,2048]{4,1,3,2,0:T(2,128)(2,1)}), bf16[32,2,1,10,2048]{4,1,3,2,0:T(2,128)(2,1)S(1)}, u32[]{:S(2)}, u32[]{:S(2)}) async-start(bf16[32,2,1,10,2048]{4,1,3,2,0:T(2,128)(2,1)} %copy.18), calls=%async_computation.4 | async-start | bytes 5242880 | tf_op jit(solution)/shard_map/all_to_all | solution.py:29
  60.2 0.3 fusion.12
  60.5 0.2 and.96
  60.7 4.7 %scatter_custom_fusion.1 = s32[1024]{0:T(1024)} fusion(s32[640]{0:T(1024)S(1)} %get-tuple-element.8, s32[640]{0:T(1024)S(1)} %get-tuple-element.25, s32[]{:T(128)} %constant.35.clone.1), kind=kCustom, calls=%fused_computation.102 | custom fusion | bytes 4100 | tf_op jit(solution)/shard_map/scatter | solution.py:152
  65.3 53.8 %all-to-all-done.4 = bf16[32,2,1,10,2048]{4,1,3,2,0:T(2,128)(2,1)S(1)} async-done(((bf16[32,2,1,10,2048]{4,1,3,2,0:T(2,128)(2,1)}), bf16[32,2,1,10,2048]{4,1,3,2,0:T(2,128)(2,1)S(1)}, u32[]{:S(2)}, u32[]{:S(2)}) %all-to-all-start.4) | async-done | bytes 2621472 | tf_op jit(solution)/shard_map/all_to_all | solution.py:29
  119.1 4.2 %all-to-all-start.2 = ((s32[4,1,256]{2,1,0:T(1,128)}), s32[4,1,256]{2,1,0:T(1,128)S(1)}, u32[]{:S(2)}, u32[]{:S(2)}) async-start(s32[4,1,256]{2,1,0:T(1,128)} %bitcast.3), calls=%async_computation.2 | async-start | bytes 8192 | tf_op jit(solution)/shard_map/all_to_all | solution.py:162
  123.3 3.3 %copy.19 = bf16[32,2,1,10,2048]{4,3,1,0,2:T(8,128)(2,1)} copy(bf16[32,2,1,10,2048]{4,1,3,2,0:T(2,128)(2,1)S(1)} %all-to-all-done.4) | data formatting | bytes 5242880 | tf_op jit(solution)/shard_map/all_to_all | solution.py:29
  126.6 4.1 %reshape.474 = bf16[640,2048]{1,0:T(8,128)(2,1)S(1)} reshape(bf16[32,2,1,10,2048]{4,3,1,0,2:T(8,128)(2,1)} %copy.19) | data formatting | bytes 5242880 | tf_op jit(solution)/shard_map/reshape;reshape;reshape | solution.py:138
  130.7 9.4 %scatter_custom_fusion.3 = bf16[1024,2048]{1,0:T(8,128)(2,1)} fusion(s32[640]{0:T(1024)S(1)} %get-tuple-element.8, bf16[640,2048]{1,0:T(8,128)(2,1)S(1)} %reshape.474, bf16[]{:T(256)} %constant.88.clone.1), kind=kCustom, calls=%fused_computation.22 | custom fusion | bytes 4194306 | tf_op jit(solution)/shard_map/scatter | solution.py:147
  140.1 5.2 %all-to-all-start.5 = ((bf16[4,256,2048]{2,1,0:T(8,128)(2,1)}), bf16[4,256,2048]{2,1,0:T(8,128)(2,1)}, u32[]{:S(2)}, u32[]{:S(2)}) async-start(bf16[4,256,2048]{2,1,0:T(8,128)(2,1)} %bitcast.51), calls=%async_computation.5 | async-start | bytes 8388608 | tf_op jit(solution)/shard_map/all_to_all | solution.py:155
  145.3 0.4 fusion.3
  145.7 6.1 %gather_fusion.1 = bf16[1024,2048]{1,0:T(8,128)(2,1)} fusion(bf16[384,2048]{1,0:T(8,128)(2,1)S(1)} %copy-done.1, s32[1024]{0:T(1024)S(1)} %broadcast_clamp_fusion), kind=kCustom, calls=%fused_computation.1 | custom fusion | bytes 8392704 | tf_op jit(solution)/shard_map/gather | solution.py:75
  151.8 6.9 %gather_fusion.2 = f32[1024]{0:T(1024)S(1)} fusion(f32[384]{0:T(512)S(1)} %fusion.3, s32[1024]{0:T(1024)S(1)} %broadcast_clamp_fusion), kind=kCustom, calls=%fused_computation.2 | custom fusion | bytes 12288 | tf_op jit(solution)/shard_map/gather | solution.py:79
  158.7 31.0 %all-to-all-done.5 = bf16[4,256,2048]{2,1,0:T(8,128)(2,1)} async-done(((bf16[4,256,2048]{2,1,0:T(8,128)(2,1)}), bf16[4,256,2048]{2,1,0:T(8,128)(2,1)}, u32[]{:S(2)}, u32[]{:S(2)}) %all-to-all-start.5) | async-done | bytes 4194336 | tf_op jit(solution)/shard_map/all_to_all | solution.py:155
  189.6 5.2 %fusion = (f32[1024]{0:T(1024)S(1)}, f32[1024]{0:T(1024)S(1)}) fusion(bf16[1024,2048]{1,0:T(8,128)(2,1)} %gather_fusion.1, bf16[4,256,2048]{2,1,0:T(8,128)(2,1)} %all-to-all-done.5), kind=kLoop, calls=%fused_computation.15 | loop fusion | flops 12580864 | bytes 8396800 | tf_op jit(solution)/shard_map/sd,sd->s/dot_general | solution.py:76
  194.8 8.6 %select_reduce_fusion = f32[1024]{0:T(1024)S(1)} fusion(bf16[1024,2048]{1,0:T(8,128)(2,1)} %bitcast.7, f32[1024]{0:T(1024)S(1)} %get-tuple-element.27, s32[1024]{0:T(1024)S(1)} %bitcast.54, pred[1024]{0:T(1024)(128)(4,1)S(1)} %get-tuple-element.11), kind=kOutput, calls=%fused_computation.17 | convolution fusion | flops 4303354880 | bytes 4207616 | tf_op jit(solution)/shard_map/dot_general | solution.py:98
  203.4 0.7 fusion.7
  204.1 6.9 %gather_fusion.3 = f32[1024]{0:T(1024)S(1)} fusion(f32[384]{0:T(512)S(1)} %get-tuple-element.5, s32[1024]{0:T(1024)S(1)} %broadcast_clamp_fusion), kind=kCustom, calls=%fused_computation.3 | custom fusion | bytes 12288 | tf_op jit(solution)/shard_map/gather | solution.py:95
  211.0 6.9 %gather_fusion.4 = f32[1024]{0:T(1024)S(1)} fusion(f32[384]{0:T(512)S(1)} %subtract_maximum_fusion, s32[1024]{0:T(1024)S(1)} %broadcast_clamp_fusion), kind=kCustom, calls=%fused_computation.4 | custom fusion | bytes 12288 | tf_op jit(solution)/shard_map/gather | solution.py:95
  218.0 0.6 all_to_all.44
  218.6 3.2 %all-to-all-start.6 = ((f32[4,1,512]{2,1,0:T(1,128)}), f32[4,1,512]{2,1,0:T(1,128)S(1)}, u32[]{:S(2)}, u32[]{:S(2)}) async-start(f32[4,1,512]{2,1,0:T(1,128)} %all_to_all.44), calls=%async_computation.6 | async-start | bytes 16384 | tf_op jit(solution)/shard_map/all_to_all | solution.py:47
  221.9 4.1 %all-to-all-done.6 = f32[4,1,512]{2,1,0:T(1,128)S(1)} async-done(((f32[4,1,512]{2,1,0:T(1,128)}), f32[4,1,512]{2,1,0:T(1,128)S(1)}, u32[]{:S(2)}, u32[]{:S(2)}) %all-to-all-start.6) | async-done | bytes 8224 | tf_op jit(solution)/shard_map/all_to_all | solution.py:47
  226.0 2.8 %gather_fusion.5 = f32[640]{0:T(1024)S(1)} fusion(f32[1024]{0:T(1024)S(1)} %bitcast.50, s32[1024]{0:T(1024)S(1)} %pad_clamp_fusion.1), kind=kCustom, calls=%fused_computation.5 | custom fusion | bytes 7680 | tf_op jit(solution)/shard_map/gather | solution.py:181
  228.9 2.8 %gather_fusion.6 = f32[640]{0:T(1024)S(1)} fusion(f32[1024]{0:T(1024)S(1)} %bitcast.49, s32[1024]{0:T(1024)S(1)} %pad_clamp_fusion.1), kind=kCustom, calls=%fused_computation.6 | custom fusion | bytes 7680 | tf_op jit(solution)/shard_map/gather | solution.py:182
  231.8 0.7 pad_maximum_fusion
  232.5 14.1 %all-to-all-start.7 = ((f32[64,1,20]{2,1,0:T(1,128)}), f32[64,1,20]{2,1,0:T(1,128)S(1)}, u32[]{:S(2)}, u32[]{:S(2)}) async-start(f32[64,1,20]{2,1,0:T(1,128)} %bitcast.13), calls=%async_computation.7 | async-start | bytes 65536 | tf_op jit(solution)/shard_map/all_to_all | solution.py:47
  246.7 9.3 %all-to-all-done.7 = f32[64,1,20]{2,1,0:T(1,128)S(1)} async-done(((f32[64,1,20]{2,1,0:T(1,128)}), f32[64,1,20]{2,1,0:T(1,128)S(1)}, u32[]{:S(2)}, u32[]{:S(2)}) %all-to-all-start.7) | async-done | bytes 5152 | tf_op jit(solution)/shard_map/all_to_all | solution.py:47
  256.3 3.4 %gather_fusion.7 = f32[512]{0:T(512)} fusion(f32[640]{0:T(1024)S(1)} %reshape.371, s32[1024]{0:T(1024)S(1)} %pad_clamp_fusion), kind=kCustom, calls=%fused_computation.7 | custom fusion | bytes 6144 | tf_op jit(solution)/shard_map/gather | solution.py:190
  259.7 3.4 %gather_fusion.8 = f32[512]{0:T(512)} fusion(f32[640]{0:T(1024)S(1)} %reshape.372, s32[1024]{0:T(1024)S(1)} %pad_clamp_fusion), kind=kCustom, calls=%fused_computation.8 | custom fusion | bytes 6144 | tf_op jit(solution)/shard_map/gather | solution.py:191
  (52 shorter events, 2.3 us)
Async XLA Ops:
  0.6 1.0 copy-start
  9.7 19.8 %all-to-all-start = ((s32[2,1,320]{2,1,0:T(1,128)}), s32[2,1,320]{2,1,0:T(1,128)S(1)}, u32[]{:S(2)}, u32[]{:S(2)}) async-start(s32[2,1,320]{2,1,0:T(1,128)} %reshape.498), calls=%async_computation | async-start | bytes 6144 | tf_op jit(solution)/shard_map/all_to_all | solution.py:29
  29.5 6.7 %all-to-all-start.3 = ((bf16[32,2,1,10,2048]{4,0,3,2,1:T(8,128)(2,1)}), bf16[32,2,1,10,2048]{4,0,3,2,1:T(8,128)(2,1)S(1)}, u32[]{:S(2)}, u32[]{:S(2)}) async-start(bf16[32,2,1,10,2048]{4,0,3,2,1:T(8,128)(2,1)} %copy.17), calls=%async_computation.3 | async-start | bytes 5242880 | tf_op jit(solution)/shard_map/all_to_all | solution.py:29
  36.3 18.1 %all-to-all-start.1 = ((s32[32,2,1,10]{3,1,2,0:T(2,128)}), s32[32,2,1,10]{3,1,2,0:T(2,128)S(1)}, u32[]{:S(2)}, u32[]{:S(2)}) async-start(s32[32,2,1,10]{3,1,2,0:T(2,128)} %copy.16), calls=%async_computation.1 | async-start | bytes 65536 | tf_op jit(solution)/shard_map/all_to_all | solution.py:29
  54.4 64.7 %all-to-all-start.4 = ((bf16[32,2,1,10,2048]{4,1,3,2,0:T(2,128)(2,1)}), bf16[32,2,1,10,2048]{4,1,3,2,0:T(2,128)(2,1)S(1)}, u32[]{:S(2)}, u32[]{:S(2)}) async-start(bf16[32,2,1,10,2048]{4,1,3,2,0:T(2,128)(2,1)} %copy.18), calls=%async_computation.4 | async-start | bytes 5242880 | tf_op jit(solution)/shard_map/all_to_all | solution.py:29
  119.1 21.0 %all-to-all-start.2 = ((s32[4,1,256]{2,1,0:T(1,128)}), s32[4,1,256]{2,1,0:T(1,128)S(1)}, u32[]{:S(2)}, u32[]{:S(2)}) async-start(s32[4,1,256]{2,1,0:T(1,128)} %bitcast.3), calls=%async_computation.2 | async-start | bytes 8192 | tf_op jit(solution)/shard_map/all_to_all | solution.py:162
  140.1 5.2 %copy-start.1 = (bf16[384,2048]{1,0:T(8,128)(2,1)S(1)}, bf16[384,2048]{1,0:T(8,128)(2,1)}, u32[]{:S(2)}) copy-start(bf16[384,2048]{1,0:T(8,128)(2,1)} %param.6) | copy-start | bytes 4718596
  140.1 49.6 %all-to-all-start.5 = ((bf16[4,256,2048]{2,1,0:T(8,128)(2,1)}), bf16[4,256,2048]{2,1,0:T(8,128)(2,1)}, u32[]{:S(2)}, u32[]{:S(2)}) async-start(bf16[4,256,2048]{2,1,0:T(8,128)(2,1)} %bitcast.51), calls=%async_computation.5 | async-start | bytes 8388608 | tf_op jit(solution)/shard_map/all_to_all | solution.py:155
  204.1 13.8 %copy-start.2 = (f32[3,384]{1,0:T(4,128)}, f32[3,384]{1,0:T(4,128)S(1)}, u32[]{:S(2)}) copy-start(f32[3,384]{1,0:T(4,128)S(1)} %fusion.7) | copy-start | bytes 13828
  218.6 7.4 %all-to-all-start.6 = ((f32[4,1,512]{2,1,0:T(1,128)}), f32[4,1,512]{2,1,0:T(1,128)S(1)}, u32[]{:S(2)}, u32[]{:S(2)}) async-start(f32[4,1,512]{2,1,0:T(1,128)} %all_to_all.44), calls=%async_computation.6 | async-start | bytes 16384 | tf_op jit(solution)/shard_map/all_to_all | solution.py:47
  232.5 23.5 %all-to-all-start.7 = ((f32[64,1,20]{2,1,0:T(1,128)}), f32[64,1,20]{2,1,0:T(1,128)S(1)}, u32[]{:S(2)}, u32[]{:S(2)}) async-start(f32[64,1,20]{2,1,0:T(1,128)} %bitcast.13), calls=%async_computation.7 | async-start | bytes 65536 | tf_op jit(solution)/shard_map/all_to_all | solution.py:47
where the time goes:
time: 264 us; the launch traced here: 263 us
  waiting for transfers between devices  104 us (39%)
  local copies, waits for them, and re-layouts  88.5 us (34%)
  starting transfers between devices  51 us (19%)
  matrix products  9.8 us (4%)
  other arithmetic  8.74 us (3%)
    all_to_all x4, waiting for transfers between devices, moved_by_axis(): lax.all_to_all(blocks, axes[k], split_axis=k, concat_axis=k, tiled=True)  59.8 us
    all_to_all x1, waiting for transfers between devices, local(): lax.all_to_all(forward.reshape(cent_count, inner_cap, width), 'cent', spl...  31 us
    all_to_all x4, starting transfers between devices, moved_by_axis(): lax.all_to_all(blocks, axes[k], split_axis=k, concat_axis=k, tiled=True)  24.3 us
    all_to_all x2, starting transfers between devices, sent_together(): lax.all_to_all(both, axis, split_axis=split_dim, concat_axis=concat_dim,...  17.4 us
    all_to_all x2, waiting for transfers between devices, sent_together(): lax.all_to_all(both, axis, split_axis=split_dim, concat_axis=concat_dim,...  13.4 us
    scatter x1, local copies, waits for them, and re-layouts, local(): forward = jnp.zeros((cent_count * inner_cap, width), jnp.bfloat16).at[sec...  9.4 us
    dot_general x1, matrix products, owner_work(): lax.dot_general(incoming, incoming, (((1,), (1,)), ((), ())), preferred_e...  8.55 us
    all_to_all x3, local copies, waits for them, and re-layouts, moved_by_axis(): lax.all_to_all(blocks, axes[k], split_axis=k, concat_axis=k, tiled=True)  8.24 us
  transfers between devices with their start and end apart: 8, of which 6 were waited for; matrix products, arithmetic and copies ran while one was open for 21% of the time, Pallas kernels for 0%

commit v1 on v0

v1 whole, which is shorter than its diff:
```python
import math

import jax
import jax.numpy as jnp
from jax import lax
from jax.experimental import pallas as pl
from jax.experimental.pallas import tpu as pltpu
from jax.sharding import Mesh
from jax.sharding import PartitionSpec as P

AXES = ("dp_0", "dp_1", "dp_2", "cent")
MESH = pl.DeviceIdType.MESH
F32 = jnp.float32
BF16 = jnp.bfloat16
HIGHEST = lax.Precision.HIGHEST

NX, NZ, NK, NY = 4, 8, 2, 4
NJ = NX * NK
GROUPS = NZ * NJ
MAIN, SPILL, CAP = 8, 2, 4
STEPS = (0, 4, 3, 5, 2, 6, 1, 7)
ROWS = NJ * CAP
BLOCK = NY * ROWS


def dot(a, b, dims=((1,), (0,)), precision=None):
    return lax.dot_general(a, b, (dims, ((), ())), precision=precision, preferred_element_type=F32)


def iota(shape, dim):
    return lax.broadcasted_iota(jnp.int32, shape, dim)


def fiota(shape, dim):
    return iota(shape, dim).astype(F32)


def rsum(value, axis):
    return jnp.sum(value, axis=axis, keepdims=True)


def rmax(value, axis):
    return jnp.max(value, axis=axis, keepdims=True)


def one_if(mask, dtype=F32):
    return jnp.where(mask, 1.0, 0.0).astype(dtype)


def kernel(
    slot_ref, docs_hbm, cents_hbm,
    proto_ref, red_ref, stats_ref,
    docs, cents, out, inbox, fwd, block,
    tag_out, tag_in, own_out, own_in,
    assign, place, qcol, tags, rowscale, rowtag, simil, best, rowbest, tot,
    score, score_in, reply, reply_in,
    load_sem, doc_send, doc_recv, tag_send, tag_recv, own_send, own_recv,
    fwd_send, fwd_recv, score_send, score_recv, reply_send, reply_recv,
):
    x, z, k, y = (lax.axis_index(a) for a in AXES)
    count, width = docs.shape
    table = cents.shape[0]
    quarter = width // 4
    me_j = x * NK + k

    load_docs = pltpu.make_async_copy(docs_hbm, docs, load_sem.at[0])
    load_cents = pltpu.make_async_copy(cents_hbm, cents, load_sem.at[1])
    load_docs.start()
    load_cents.start()

    def peer(dz, t):
        px = lax.rem(x + t // NK, NX)
        pk = lax.rem(k + lax.rem(t, NK), NK)
        pz = lax.rem(z + dz, NZ)
        return px, pz, pk

    barrier = pltpu.get_barrier_semaphore()

    def greet(t, carry):
        px, pz, pk = peer(t // NJ, lax.rem(t, NJ))
        pl.semaphore_signal(barrier, inc=1, device_id=(px, pz, pk, y), device_id_type=MESH)
        return carry

    lax.fori_loop(1, GROUPS, greet, 0)
    for dy in range(1, NY):
        pl.semaphore_signal(
            barrier, inc=1, device_id=(x, z, k, lax.rem(y + dy, NY)), device_id_type=MESH
        )

    slot = slot_ref[...].astype(F32)
    owner = jnp.floor((slot + 0.5) * (1.0 / table))
    local = slot - owner * table
    row = jnp.floor(owner * (1.0 / NY))
    col = owner - row * NY
    dest_x = jnp.floor(row * (1.0 / (NZ * NK)))
    rest = row - dest_x * (NZ * NK)
    dest_z = jnp.floor(rest * (1.0 / NK))
    dest_k = rest - dest_z * NK
    step = dest_z - z.astype(F32)
    step = jnp.where(step < 0.0, step + NZ, step)
    order = jnp.zeros_like(step)
    for n, dz in enumerate(STEPS):
        order = jnp.where(step == float(dz), float(n), order)
    col = col - y.astype(F32)
    col = jnp.where(col < 0.0, col + NY, col)
    group = order * NJ + dest_x * NK + dest_k
    at_group = one_if(fiota((GROUPS, count), 0) == group)
    at_owner = one_if(fiota((GROUPS * NY, count), 0) == group * NY + col)
    earlier = one_if(iota((count, count), 0) < iota((count, count), 1), BF16)
    rank = rsum(dot(at_group.astype(BF16), earlier) * at_group, 0)
    rank_owner = rsum(dot(at_owner.astype(BF16), earlier) * at_owner, 0)
    is_main = rank < float(MAIN)
    main_at = jnp.where(is_main, group * MAIN + rank, -1.0)
    spill_at = jnp.where(is_main, -8.0, group * MAIN + (rank - MAIN) * 4.0)
    assign[...] = at_group
    place[...] = col * (2.0 * CAP) + rank_owner

    jf = me_j.astype(F32)
    value = col * float(ROWS) + jf * CAP + rank_owner + 1.0
    lane = fiota((128, count), 0)
    main_lane = jnp.where(is_main, jf * MAIN + rank, -8.0)
    spill_lane = jnp.where(is_main, -8.0, 64.0 + jf * MAIN + (rank - MAIN) * 4.0)
    hit = (lane == main_lane) | ((lane >= spill_lane) & (lane < spill_lane + 4.0))
    first = dot(at_group.astype(BF16), jnp.where(hit, value, 0.0).astype(BF16), ((1,), (1,)))
    hit = lane == value - 1.0
    high = jnp.floor((local + 1.0) * (1.0 / 16.0))
    low = local + 1.0 - high * 16.0
    second = 16.0 * dot(at_group.astype(BF16), jnp.where(hit, high, 0.0).astype(BF16), ((1,), (1,)))
    second += dot(at_group.astype(BF16), jnp.where(hit, low, 0.0).astype(BF16), ((1,), (1,)))
    both = jnp.concatenate([first, second], axis=1)
    for g in range(GROUPS):
        tag_out[g] = both[g : g + 1, :]
    tag_in[me_j] = tag_out[me_j]

    load_docs.wait()

    half = GROUPS // 2

    def pack(h):
        at = fiota((half * MAIN, count), 0) + float(h * half * MAIN)
        pick = one_if(at == main_at, BF16)
        for q in range(4):
            cols = slice(q * quarter, (q + 1) * quarter)
            packed = dot(pick, docs[:, cols]).astype(BF16)
            out[h * half : (h + 1) * half, :, cols] = packed.reshape(half, MAIN, quarter)
        spilled = jnp.zeros((half * MAIN, quarter), F32)
        for q in range(4):
            cols = slice(q * quarter, (q + 1) * quarter)
            spilled += dot(one_if(at == spill_at + float(q), BF16), docs[:, cols])
        out[h * half : (h + 1) * half, :, width:] = spilled.astype(BF16).reshape(half, MAIN, quarter)

    def send_docs(n):
        dz = STEPS[n]

        def body(t, carry):
            px, pz, pk = peer(dz, t)
            pltpu.make_async_remote_copy(
                src_ref=out.at[n * NJ + px * NK + pk],
                dst_ref=inbox.at[n * NJ + me_j],
                send_sem=doc_send.at[n],
                recv_sem=doc_recv.at[n],
                device_id=(px, pz, pk, y),
                device_id_type=MESH,
            ).start()
            return carry

        lax.fori_loop(1 if dz == 0 else 0, NJ, body, 0)

    def arrived(ref, sem):
        pltpu.make_async_copy(ref, ref, sem).wait()

    def y_send(dy, src, dst, send, recv):
        return pltpu.make_async_remote_copy(
            src_ref=src, dst_ref=dst, send_sem=send, recv_sem=recv,
            device_id=(x, z, k, lax.rem(y + dy, NY)), device_id_type=MESH,
        )

    pack(0)
    pl.semaphore_wait(barrier, GROUPS - 1 + NY - 1)

    for n, dz in enumerate(STEPS):

        def send_tag(t, carry, n=n, dz=dz):
            px, pz, pk = peer(dz, t)
            pltpu.make_async_remote_copy(
                src_ref=tag_out.at[n * NJ + px * NK + pk],
                dst_ref=tag_in.at[n * NJ + me_j],
                send_sem=tag_send,
                recv_sem=tag_recv,
                device_id=(px, pz, pk, y),
                device_id_type=MESH,
            ).start()
            return carry

        lax.fori_loop(1 if dz == 0 else 0, NJ, send_tag, 0)

    for n in range(NZ // 2):
        send_docs(n)
    inbox[me_j] = out[me_j]
    pack(1)
    load_cents.wait()

    squares = jnp.zeros((table, 128), F32)
    for c in range(width // 128):
        part = cents[:, c * 128 : (c + 1) * 128].astype(F32)
        squares += part * part
    qcol[...] = lax.rsqrt(rsum(squares, 1) + 1.0)

    for n in range(NZ // 2, NZ):
        send_docs(n)

    arrived(tag_in.at[pl.ds(0, GROUPS - 1)], tag_recv)
    for n in range(NZ):
        own = tag_in[n * NJ]
        for j in range(1, NJ):
            own += tag_in[n * NJ + j]
        own_out[n : n + 1, :] = own
    for dy in range(1, NY):
        y_send(dy, own_out, own_in.at[dy], own_send, own_recv).start()
    own_in[0] = own_out[...]

    tot[...] = jnp.zeros_like(tot)
    best[...] = jnp.zeros_like(best)
    rowbest[...] = jnp.zeros_like(rowbest)

    def relay(n, in_groups):
        in_groups()
        marks = own_out[pl.ds(n, 1), :]
        target = fiota((BLOCK, 64), 0) + 1.0
        pick = one_if(target == marks[:, :64], BF16)
        spill = target == marks[:, 64:128]
        phase = lax.rem(iota((BLOCK, 64), 1), 4)
        got = inbox[pl.ds(n * NJ, NJ)].reshape(64, width + quarter)
        for q in range(4):
            cols = slice(q * quarter, (q + 1) * quarter)
            rows = dot(pick, got[:, cols])
            rows += dot(one_if(spill & (phase == q), BF16), got[:, width:])
            rows = rows.astype(BF16)
            block[n, :ROWS, cols] = rows[:ROWS]
            fwd[n, :, cols] = rows[ROWS:]
        for dy in range(1, NY):
            y_send(
                dy,
                fwd.at[n, pl.ds((dy - 1) * ROWS, ROWS)],
                block.at[n, pl.ds(dy * ROWS, ROWS)],
                fwd_send.at[n],
                fwd_recv.at[n],
            ).start()

    eye = iota((BLOCK, BLOCK), 0) == iota((BLOCK, BLOCK), 1)
    source = iota((NZ, 128), 1) // ROWS

    def owner_block(n):
        arrived(block.at[n, pl.ds(0, BLOCK - ROWS)], fwd_recv.at[n])
        mine = block[n]
        tag = tags[pl.ds(n, 1), :]
        gram = dot(mine, mine, ((1,), (1,)))
        square = jnp.where(eye, gram, 0.0)
        scale = lax.rsqrt(rsum(square, 0) + 1.0)
        scale_col = lax.rsqrt(rsum(square, 1) + 1.0)
        tag_col = rsum(jnp.where(eye, jnp.broadcast_to(tag, (BLOCK, BLOCK)), 0.0), 1)
        rowscale[n] = jnp.broadcast_to(scale_col, (BLOCK, BLOCK))
        rowtag[n] = jnp.broadcast_to(tag_col, (BLOCK, BLOCK))
        live = tag > 0.0
        pair = jnp.where((tag_col == tag) & live & jnp.logical_not(eye), gram, 0.0)
        top = rmax(pair * scale_col, 0)

        def earlier_block(m, top):
            other = dot(block[m], mine, ((1,), (1,)))
            pair = jnp.where((rowtag[m] == tag) & live, other, 0.0)
            rowbest[m] = jnp.maximum(rowbest[m], pair * scale)
            return jnp.maximum(top, rmax(pair * rowscale[m], 0))

        top = lax.fori_loop(0, n, earlier_block, top)
        best[pl.ds(n, 1), :] = top * scale

        cross = dot(cents[...], mine, ((1,), (1,)))
        member = (fiota((table, BLOCK), 0) + 1.0) == tag
        similar = rsum(jnp.where(member, cross * qcol[...], 0.0), 0) * scale
        simil[pl.ds(n, 1), :] = similar
        tot[0] += one_if(member)
        tot[1] += jnp.where(member, similar, 0.0)
        tot[2] += jnp.where(member, similar * similar, 0.0)

    def doc_wait(n, count):
        arrived(inbox.at[pl.ds(0, count)], doc_recv.at[n])

    relay(0, lambda: doc_wait(0, NJ - 1))
    arrived(own_in.at[pl.ds(1, NY - 1)], own_recv)
    mix = jnp.zeros((NZ, 128), F32)
    for dy in range(NY):
        mix = jnp.where(source == dy, own_in[dy, :, 128:], mix)
    tags[...] = mix

    def main_step(n, carry):
        relay(n, lambda: doc_wait(n, NJ))
        owner_block(n - 1)
        return carry

    lax.fori_loop(1, NZ, main_step, 0)
    owner_block(NZ - 1)

    counts = rsum(tot[0], 1)
    sums = rsum(tot[1], 1)
    squares = rsum(tot[2], 1)
    pos = iota((table, 128), 1)
    stacked = jnp.where(pos == 0, counts, jnp.where(pos == 1, sums, jnp.where(pos == 2, squares, 0.0)))
    stats_ref[...] = stacked.T[:3]
    floor = jnp.maximum(counts, 1.0)
    mean = sums / floor
    spread = jnp.sqrt(jnp.maximum(squares / floor - mean * mean, 0.0) + 1.0 / width)

    def scores(n, carry):
        tag = tags[pl.ds(n, 1), :]
        member = (fiota((table, BLOCK), 0) + 1.0) == tag
        mean_at = rsum(jnp.where(member, mean, 0.0), 0)
        spread_at = rsum(jnp.where(member, spread, 0.0), 0)
        gap = (mean_at - simil[pl.ds(n, 1), :]) / jnp.where(tag > 0.0, spread_at, 1.0)
        score[0, pl.ds(n, 1), :] = jnp.where(tag > 0.0, gap, 0.0)
        rows = rmax((rowbest[n] * rowscale[n]).T, 0)
        score[1, pl.ds(n, 1), :] = math.sqrt(width) * jnp.maximum(best[pl.ds(n, 1), :], rows)
        return carry

    lax.fori_loop(0, NZ, scores, 0)
    for dy in range(1, NY):
        y_send(NY - dy, score, score_in.at[dy], score_send, score_recv).start()
    score_in[0] = score[...]

    arrived(score_in.at[pl.ds(1, NY - 1)], score_recv)
    lanes = iota((GROUPS, 128), 1)
    mine = lax.rem(lanes, ROWS) // CAP == lax.rem(iota((GROUPS, 128), 0), NJ)
    from_lane, to_lane = iota((128, 128), 0), iota((128, 128), 1)
    laid = jnp.zeros((GROUPS, 128), F32)
    for s in range(2):
        held = jnp.zeros((NZ, 128), F32)
        for dy in range(NY):
            held = jnp.where(source == dy, score_in[dy, s], held)
        held = jnp.broadcast_to(held[:, None, :], (NZ, NJ, 128)).reshape(GROUPS, 128)
        move = one_if(to_lane == (from_lane // ROWS) * (2 * CAP) + s * CAP + lax.rem(from_lane, CAP))
        laid += dot(jnp.where(mine, held, 0.0), move, precision=HIGHEST)
    for g in range(GROUPS):
        reply[g] = laid[g : g + 1, :]

    for n, dz in enumerate(STEPS):

        def send_reply(t, carry, n=n, dz=dz):
            px, pz, pk = peer(NZ - dz, t)
            pltpu.make_async_remote_copy(
                src_ref=reply.at[n * NJ + px * NK + pk],
                dst_ref=reply_in.at[n * NJ + me_j],
                send_sem=reply_send,
                recv_sem=reply_recv,
                device_id=(px, pz, pk, y),
                device_id_type=MESH,
            ).start()
            return carry

        lax.fori_loop(1 if dz == 0 else 0, NJ, send_reply, 0)
    reply_in[me_j] = reply[me_j]
    arrived(reply_in.at[pl.ds(0, GROUPS - 1)], reply_recv)
    home = jnp.concatenate(
        [reply_in[...].reshape(GROUPS, 128), jnp.zeros((128 - GROUPS, 128), F32)], axis=0
    ).T
    picked = dot(home[: NY * 2 * CAP, :GROUPS], assign[...], precision=HIGHEST)
    at = fiota((NY * 2 * CAP, count), 0)
    proto_ref[...] = rsum(jnp.where(at == place[...], picked, 0.0), 0)
    red_ref[...] = rsum(jnp.where(at == place[...] + CAP, picked, 0.0), 0)

    for n, dz in enumerate(STEPS):
        arrived(inbox.at[pl.ds(0, NJ - 1 if dz == 0 else NJ)], doc_send.at[n])
        arrived(fwd.at[n], fwd_send.at[n])
    arrived(tag_out.at[pl.ds(0, GROUPS - 1)], tag_send)
    arrived(reply.at[pl.ds(0, GROUPS - 1)], reply_send)
    arrived(own_in.at[pl.ds(1, NY - 1)], own_send)
    arrived(score_in.at[pl.ds(1, NY - 1)], score_send)


def local(documents, assigned, centroids, owner_slot):
    count, width = documents.shape
    table = centroids.shape[0]
    wide = width + width // 4
    slot = owner_slot[assigned].reshape(1, count)
    dma = pltpu.SemaphoreType.DMA
    proto, red, stats = pl.pallas_call(
        kernel,
        out_shape=(
            jax.ShapeDtypeStruct((1, count), F32),
            jax.ShapeDtypeStruct((1, count), F32),
            jax.ShapeDtypeStruct((3, table), F32),
        ),
        in_specs=[
            pl.BlockSpec(memory_space=pltpu.VMEM),
            pl.BlockSpec(memory_space=pl.ANY),
            pl.BlockSpec(memory_space=pl.ANY),
        ],
        out_specs=(pl.BlockSpec(memory_space=pltpu.VMEM),) * 3,
        scratch_shapes=[
            pltpu.VMEM((count, width), BF16),
            pltpu.VMEM((table, width), BF16),
            pltpu.VMEM((GROUPS, MAIN, wide), BF16),
            pltpu.VMEM((GROUPS, MAIN, wide), BF16),
            pltpu.VMEM((NZ, BLOCK - ROWS, width), BF16),
            pltpu.VMEM((NZ, BLOCK, width), BF16),
            pltpu.VMEM((GROUPS, 1, 256), F32),
            pltpu.VMEM((GROUPS, 1, 256), F32),
            pltpu.VMEM((NZ, 256), F32),
            pltpu.VMEM((NY, NZ, 256), F32),
            pltpu.VMEM((GROUPS, count), F32),
            pltpu.VMEM((1, count), F32),
            pltpu.VMEM((table, 1), F32),
            pltpu.VMEM((NZ, BLOCK), F32),
            pltpu.VMEM((NZ, BLOCK, BLOCK), F32),
            pltpu.VMEM((NZ, BLOCK, BLOCK), F32),
            pltpu.VMEM((NZ, BLOCK), F32),
            pltpu.VMEM((NZ, BLOCK), F32),
            pltpu.VMEM((NZ, BLOCK, BLOCK), F32),
            pltpu.VMEM((3, table, BLOCK), F32),
            pltpu.VMEM((2, NZ, BLOCK), F32),
            pltpu.VMEM((NY, 2, NZ, BLOCK), F32),
            pltpu.VMEM((GROUPS, 1, 128), F32),
            pltpu.VMEM((GROUPS, 1, 128), F32),
            dma((2,)),
            dma((NZ,)), dma((NZ,)),
            dma, dma,
            dma, dma,
            dma((NZ,)), dma((NZ,)),
            dma, dma,
            dma, dma,
        ],
        compiler_params=pltpu.CompilerParams(
            collective_id=0, has_side_effects=True, vmem_limit_bytes=56 * 1024 * 1024
        ),
        name="route_and_score",
    )(slot, documents, centroids)
    return proto.reshape(count), red.reshape(count), stats


def solution(mesh):
    split = Mesh(mesh.devices.reshape(NX, NZ, NK, NY), AXES)
    placed = (P(AXES, None), P(AXES), P(AXES, None), P())
    return jax.shard_map(
        local,
        mesh=split,
        in_specs=placed,
        out_specs=(P(AXES), P(AXES), P(None, AXES)),
        check_vma=False,
    )
```

time: 264 us -> 119 us (0.45)
  Pallas kernels: 0 us -> 109 us
  waiting for transfers between devices: 104 us -> 0 us
  local copies, waits for them, and re-layouts: 88.5 us -> 8.3 us
  starting transfers between devices: 51 us -> 0 us
  matrix products: 9.8 us -> 0 us
  other arithmetic: 8.74 us -> 0.74 us
    pallas_call x0 -> x1, Pallas kernels: none -> 109 us  [local(): pl.pallas_call(kernel, out_shape=(jax.ShapeDtypeStruct((1, count), F32),...]
    all_to_all x8 -> x0, waiting for transfers between devices: 104 us -> none  [the longest x4 59.8 us: moved_by_axis(): lax.all_to_all(blocks, axes[k], split_axis=k, concat_axis=k, tiled=True)]
    all_to_all x8 -> x0, starting transfers between devices: 51 us -> none  [the longest x4 24.3 us: moved_by_axis(): lax.all_to_all(blocks, axes[k], split_axis=k, concat_axis=k, tiled=True)]
    gather x11 -> x1, local copies, waits for them, and re-layouts: 42.4 us -> 4.27 us  [local(): slot = owner_slot[assigned].reshape(1, count)]
    scatter x4 -> x0, local copies, waits for them, and re-layouts: 21.9 us -> none  [the longest x1 9.4 us: local(): forward = jnp.zeros((cent_count * inner_cap, width), jnp.bfloat16).at[sec...]
    another operation x5 -> x0, local copies, waits for them, and re-layouts: 12.3 us -> none  [the longest x4 8.19 us: moved_by_axis(): blocks = blocks.reshape(*lengths, *blocks.shape[1:])]
    dot_general x4 -> x0, matrix products: 9.8 us -> none  [the longest x1 8.55 us: owner_work(): lax.dot_general(incoming, incoming, (((1,), (1,)), ((), ())), preferred_e...]
    all_to_all x4 -> x0, local copies, waits for them, and re-layouts: 8.84 us -> none  [the longest x3 8.24 us: moved_by_axis(): lax.all_to_all(blocks, axes[k], split_axis=k, concat_axis=k, tiled=True)]
  transfers between devices with their start and end apart: 8 -> 0, of which waited for: 6 -> 0; matrix products, arithmetic and copies ran while one was open for 21% -> 0% of each run, Pallas kernels for 0% -> 0%
where the time goes in v1:
time: 119 us
  Pallas kernels  109 us (92%)
  local copies, waits for them, and re-layouts  8.3 us (7%)
    pallas_call x1, Pallas kernels, local(): pl.pallas_call(kernel, out_shape=(jax.ShapeDtypeStruct((1, count), F32),...  109 us
    gather x1, local copies, waits for them, and re-layouts, local(): slot = owner_slot[assigned].reshape(1, count)  4.27 us
    unnamed x5, local copies, waits for them, and re-layouts  4.03 us

profile of v1, /device:TPU:1, one launch (start us, length us, event | category | flops | bytes accessed | tf_op | source)
XLA Modules:
  0.0 118.7 jit_solution(15105727566759641570)
XLA Ops:
  0.6 0.0 copy-start
  0.6 0.7 compare_select_fusion
  1.4 0.3 copy-done
  1.6 4.3 %gather_fusion = s32[512]{0:T(512)} fusion(s32[98304]{0:T(1024)S(1)} %copy-done, s32[1024]{0:T(1024)S(1)} %pad_clamp_fusion), kind=kCustom, calls=%fused_computation | custom fusion | bytes 6144 | tf_op jit(solution)/shard_map/gather | solution.py:382
  5.9 109.0 %route_and_score.1 = (f32[1,512]{1,0:T(1,128)}, f32[1,512]{1,0:T(1,128)}, f32[3,384]{1,0:T(4,128)}) custom-call(s32[1,512]{1,0:T(1,128)} %bitcast.3, bf16[512,2048]{1,0:T(8,128)(2,1)} %docs_hbm.1, bf16[384,2048]{1,0:T(8,128)(2,1)} %cents_hbm.1), custom_call_target="tpu_custom_call" | custom-call | tf_op jit(solution)/shard_map/route_and_score/pallas_call | solution.py:384
  114.9 1.2 %copy.10 = f32[512]{0:T(512)} copy(f32[512]{0:T(512)} %bitcast.5) | data formatting | bytes 4096
  116.1 1.2 %copy.11 = f32[512]{0:T(512)} copy(f32[512]{0:T(512)} %bitcast.4) | data formatting | bytes 4096
  117.4 1.3 %copy.12 = f32[3,384]{1,0:T(4,128)} copy(f32[3,384]{1,0:T(4,128)} %get-tuple-element.14) | data formatting | bytes 9216
  (1 shorter events, 0.0 us)
Async XLA Ops:
  0.6 1.0 copy-start

commit v2 on v1

v2 whole, which is shorter than its diff:
```python
import math

import jax
import jax.numpy as jnp
from jax import lax
from jax.experimental import pallas as pl
from jax.experimental.pallas import tpu as pltpu
from jax.sharding import Mesh
from jax.sharding import PartitionSpec as P

AXES = ("dp_0", "dp_1", "dp_2", "cent")
MESH = pl.DeviceIdType.MESH
F32 = jnp.float32
BF16 = jnp.bfloat16
HIGHEST = lax.Precision.HIGHEST

NX, NZ, NK, NY = 4, 8, 2, 4
NJ = NX * NK
GROUPS = NZ * NJ
MAIN, SPILL, CAP = 8, 2, 4
STEPS = tuple((n + 1) // 2 if n % 2 else -(n // 2) % NZ for n in range(NZ))
ROWS = NJ * CAP
BLOCK = NY * ROWS


def dot(a, b, dims=((1,), (0,)), precision=None):
    return lax.dot_general(a, b, (dims, ((), ())), precision=precision, preferred_element_type=F32)


def iota(shape, dim):
    return lax.broadcasted_iota(jnp.int32, shape, dim)


def fiota(shape, dim):
    return iota(shape, dim).astype(F32)


def rsum(value, axis):
    return jnp.sum(value, axis=axis, keepdims=True)


def rmax(value, axis):
    return jnp.max(value, axis=axis, keepdims=True)


def one_if(mask, dtype=F32):
    return jnp.where(mask, 1.0, 0.0).astype(dtype)


def kernel(
    assigned_hbm, slots_hbm, docs_hbm, cents_hbm,
    reply_in, assign, place, stats_ref,
    assigned, slots, docs, cents, out, inbox, fwd, block,
    tag_out, tag_in, own_out, own_in,
    qcol, tags, rowscale, rowtag, simil, best, rowbest, tot,
    score, score_in, reply,
    ring, load_sem, doc_send, doc_recv, tag_send, tag_recv, own_send, own_recv,
    fwd_send, fwd_recv, score_send, score_recv, reply_send, reply_recv,
):
    x, z, k, y = (lax.axis_index(a) for a in AXES)
    count, width = docs.shape
    table = cents.shape[0]
    quarter = width // 4

    load_assigned = pltpu.make_async_copy(assigned_hbm, assigned, load_sem.at[2])
    load_slots = pltpu.make_async_copy(slots_hbm, slots, load_sem.at[3])
    load_docs = pltpu.make_async_copy(docs_hbm, docs, load_sem.at[0])
    load_cents = pltpu.make_async_copy(cents_hbm, cents, load_sem.at[1])
    load_assigned.start()
    load_slots.start()
    load_docs.start()
    load_cents.start()

    def peer(dz, t, sign=1):
        px = lax.rem(x + NX + sign * (t // NK), NX)
        pk = lax.rem(k + NK + sign * lax.rem(t, NK), NK)
        pz = lax.rem(z + NZ + sign * dz, NZ)
        return px, pz, pk

    barrier = pltpu.get_barrier_semaphore()

    def hello(sem, px, pz, pk, py):
        pl.semaphore_signal(sem, inc=1, device_id=(px, pz, pk, py), device_id_type=MESH)

    above, below = lax.rem(z + 1, NZ), lax.rem(z + NZ - 1, NZ)
    hello(barrier, x, above, k, y)
    hello(barrier, x, below, k, y)
    for t in range(1, NJ):
        px, pz, pk = peer(0, t)
        hello(barrier, px, pz, pk, y)
    for dy in range(1, NY):
        hello(barrier, x, z, k, lax.rem(y + dy, NY))

    def ring_signal(r):
        hello(ring.at[r, 0], x, above, k, y)
        hello(ring.at[r, 1], x, below, k, y)

    def ring_wait(r):
        pl.semaphore_wait(ring.at[r, 0], 1)
        pl.semaphore_wait(ring.at[r, 1], 1)

    load_assigned.wait()
    load_slots.wait()
    number = assigned[...].astype(F32)
    at_row = jnp.floor(number * (1.0 / 128.0))
    at_lane = number - at_row * 128.0
    held = slots.shape[0]
    turned = jnp.concatenate(
        [slots[r * 128 : (r + 1) * 128, :].astype(F32).T for r in range(held // 128)], axis=1
    )
    top = jnp.floor(turned * (1.0 / 4096.0))
    turned -= top * 4096.0
    middle = jnp.floor(turned * (1.0 / 64.0))
    turned -= middle * 64.0
    digits = jnp.concatenate([top, middle, turned], axis=0).astype(BF16)
    digits = dot(digits, one_if(fiota((held, count), 0) == at_row, BF16))
    slot = digits[:128] * 4096.0 + digits[128:256] * 64.0 + digits[256:]
    slot = rsum(jnp.where(fiota((128, count), 0) == at_lane, slot, 0.0), 0)

    owner = jnp.floor((slot + 0.5) * (1.0 / table))
    local = slot - owner * table
    row = jnp.floor(owner * (1.0 / NY))
    col = owner - row * NY
    dest_x = jnp.floor(row * (1.0 / (NZ * NK)))
    rest = row - dest_x * (NZ * NK)
    dest_z = jnp.floor(rest * (1.0 / NK))
    dest_k = rest - dest_z * NK
    step = dest_z - z.astype(F32)
    step = jnp.where(step < 0.0, step + NZ, step)
    order = jnp.zeros_like(step)
    for n, dz in enumerate(STEPS):
        order = jnp.where(step == float(dz), float(n), order)
    col = col - y.astype(F32)
    col = jnp.where(col < 0.0, col + NY, col)
    shift_x = dest_x - x.astype(F32)
    shift_x = jnp.where(shift_x < 0.0, shift_x + NX, shift_x)
    shift_k = jnp.abs(dest_k - k.astype(F32))
    turn = shift_x * NK + shift_k
    group = order * NJ + turn
    at_group = one_if(fiota((GROUPS, count), 0) == group)
    at_owner = one_if(fiota((GROUPS * NY, count), 0) == group * NY + col)
    earlier = one_if(iota((count, count), 0) < iota((count, count), 1), BF16)
    rank = rsum(dot(at_group.astype(BF16), earlier) * at_group, 0)
    rank_owner = rsum(dot(at_owner.astype(BF16), earlier) * at_owner, 0)
    is_main = rank < float(MAIN)
    main_at = jnp.where(is_main, group * MAIN + rank, -1.0)
    spill_at = jnp.where(is_main, -8.0, group * MAIN + (rank - MAIN) * 4.0)
    assign[...] = at_group
    place[...] = col * (2.0 * CAP) + rank_owner

    value = col * float(ROWS) + turn * CAP + rank_owner + 1.0
    lane = fiota((128, count), 0)
    main_lane = jnp.where(is_main, turn * MAIN + rank, -8.0)
    spill_lane = jnp.where(is_main, -8.0, 64.0 + turn * MAIN + (rank - MAIN) * 4.0)
    hit = (lane == main_lane) | ((lane >= spill_lane) & (lane < spill_lane + 4.0))
    first = dot(at_group.astype(BF16), jnp.where(hit, value, 0.0).astype(BF16), ((1,), (1,)))
    hit = lane == value - 1.0
    high = jnp.floor((local + 1.0) * (1.0 / 16.0))
    low = local + 1.0 - high * 16.0
    second = 16.0 * dot(at_group.astype(BF16), jnp.where(hit, high, 0.0).astype(BF16), ((1,), (1,)))
    second += dot(at_group.astype(BF16), jnp.where(hit, low, 0.0).astype(BF16), ((1,), (1,)))
    both = jnp.concatenate([first, second], axis=1)
    for g in range(GROUPS):
        tag_out[g] = both[g : g + 1, :]
    tag_in[0] = tag_out[0]

    half = GROUPS // 2

    def pack(h):
        at = fiota((half * MAIN, count), 0) + float(h * half * MAIN)
        pick = one_if(at == main_at, BF16)
        for q in range(4):
            cols = slice(q * quarter, (q + 1) * quarter)
            packed = dot(pick, docs[:, cols]).astype(BF16)
            out[h * half : (h + 1) * half, :, cols] = packed.reshape(half, MAIN, quarter)
        spilled = jnp.zeros((half * MAIN, quarter), F32)
        for q in range(4):
            cols = slice(q * quarter, (q + 1) * quarter)
            spilled += dot(one_if(at == spill_at + float(q), BF16), docs[:, cols])
        out[h * half : (h + 1) * half, :, width:] = spilled.astype(BF16).reshape(half, MAIN, quarter)

    def send(ref_out, ref_in, sems, n, t, sign=1):
        px, pz, pk = peer(STEPS[n], t, sign)
        pltpu.make_async_remote_copy(
            src_ref=ref_out.at[n * NJ + t],
            dst_ref=ref_in.at[n * NJ + t],
            send_sem=sems[0],
            recv_sem=sems[1],
            device_id=(px, pz, pk, y),
            device_id_type=MESH,
        ).start()

    def send_group(ref_out, ref_in, sems, n, sign=1, first=0, last=NJ):
        def body(t, carry):
            send(ref_out, ref_in, sems, n, t, sign)
            return carry

        lax.fori_loop(max(first, 1 if n == 0 else 0), last, body, 0)

    def send_docs(n):
        odd = lax.rem(n, 2)
        dz = lax.rem(odd * ((n + 1) // 2) + (1 - odd) * (NZ - n // 2), NZ)

        def body(t, carry):
            px, pz, pk = peer(dz, t)
            pltpu.make_async_remote_copy(
                src_ref=out.at[n * NJ + t],
                dst_ref=inbox.at[n * NJ + t],
                send_sem=doc_send.at[n],
                recv_sem=doc_recv.at[n + (n // (NZ - 1)) * (t // (NJ // 2))],
                device_id=(px, pz, pk, y),
                device_id_type=MESH,
            ).start()
            return carry

        lax.fori_loop(1 if isinstance(n, int) and n == 0 else 0, NJ, body, 0)

    def send_tags(n):
        send_group(tag_out, tag_in, (tag_send, tag_recv.at[n]), n)

    def arrived(ref, sem):
        pltpu.make_async_copy(ref, ref, sem).wait()

    def y_send(dy, src, dst, send, recv):
        return pltpu.make_async_remote_copy(
            src_ref=src, dst_ref=dst, send_sem=send, recv_sem=recv,
            device_id=(x, z, k, lax.rem(y + dy, NY)), device_id_type=MESH,
        )

    load_docs.wait()
    pack(0)
    pl.semaphore_wait(barrier, NJ - 1 + NY - 1 + 2)
    ring_signal(0)
    send_tags(0)
    send_docs(0)
    ring_wait(0)
    ring_signal(1)
    for n in (1, 2):
        send_tags(n)
    for n in (1, 2):
        send_docs(n)
    inbox[0] = out[0]
    ring_wait(1)
    ring_signal(2)
    for n in (3, 4):
        send_tags(n)
    send_docs(3)
    pack(1)
    send_docs(4)
    ring_wait(2)
    ring_signal(3)
    for n in (5, 6):
        send_tags(n)
    ring_wait(3)
    send_tags(7)

    tot[...] = jnp.zeros_like(tot)
    best[...] = jnp.zeros_like(best)
    rowbest[...] = jnp.zeros_like(rowbest)

    def relay_tags(n, waited):
        arrived(tag_in.at[pl.ds(0, waited)], tag_recv.at[n])
        own = tag_in[n * NJ]
        for j in range(1, NJ):
            own += tag_in[n * NJ + j]
        own_out[n] = own
        for dy in range(1, NY):
            y_send(dy, own_out.at[n], own_in.at[dy, n], own_send, own_recv.at[n]).start()

    def relay(n, waited, sem, first=0, many=NJ):
        arrived(inbox.at[pl.ds(0, waited)], doc_recv.at[sem])
        marks = own_out[n]
        deep, tall = many * MAIN, many * CAP
        at = iota((NY * tall, deep), 0)
        target = ((at // tall) * ROWS + first * CAP + lax.rem(at, tall) + 1).astype(F32)
        pick = one_if(target == marks[:, first * MAIN : first * MAIN + deep], BF16)
        spill = target == marks[:, 64 + first * MAIN : 64 + first * MAIN + deep]
        phase = lax.rem(iota((NY * tall, deep), 1), 4)
        got = inbox[pl.ds(n * NJ + first, many)].reshape(deep, width + quarter)
        for q in range(4):
            cols = slice(q * quarter, (q + 1) * quarter)
            rows = dot(pick, got[:, cols])
            rows += dot(one_if(spill & (phase == q), BF16), got[:, width:])
            rows = rows.astype(BF16)
            block[n, first * CAP : first * CAP + tall, cols] = rows[:tall]
            for dy in range(1, NY):
                at_row = (dy - 1) * ROWS + first * CAP
                fwd[n, at_row : at_row + tall, cols] = rows[dy * tall : (dy + 1) * tall]
        for dy in range(1, NY):
            y_send(
                dy,
                fwd.at[n, pl.ds((dy - 1) * ROWS + first * CAP, tall)],
                block.at[n, pl.ds(dy * ROWS + first * CAP, tall)],
                fwd_send.at[n],
                fwd_recv.at[n],
            ).start()

    eye = iota((BLOCK, BLOCK), 0) == iota((BLOCK, BLOCK), 1)
    source = iota((1, 128), 1) // ROWS

    def owner_block(n, last=False):
        arrived(block.at[n, pl.ds(0, BLOCK - ROWS)], fwd_recv.at[n])
        mine = block[n]
        arrived(own_out.at[pl.ds(0, NY - 1)], own_recv.at[n])
        tag = own_out[n][:, 128:]
        for dy in range(1, NY):
            tag = jnp.where(source == dy, own_in[dy, n][:, 128:], tag)
        tags[pl.ds(n, 1), :] = tag
        live = tag > 0.0
        gram = dot(mine, mine, ((1,), (1,)))
        square = jnp.where(eye, gram, 0.0)
        scale = lax.rsqrt(rsum(square, 0) + 1.0)
        scale_col = lax.rsqrt(rsum(square, 1) + 1.0)
        tag_col = rsum(jnp.where(eye, jnp.broadcast_to(tag, (BLOCK, BLOCK)), 0.0), 1)
        rowscale[n] = jnp.broadcast_to(scale_col, (BLOCK, BLOCK))
        rowtag[n] = jnp.broadcast_to(tag_col, (BLOCK, BLOCK))
        pair = jnp.where((tag_col == tag) & live & jnp.logical_not(eye), gram, 0.0)
        top = rmax(pair * scale_col, 0)

        def meet(m, other, top):
            pair = jnp.where((rowtag[m] == tag) & live, other, 0.0)
            rowbest[m] = jnp.maximum(rowbest[m], pair * scale)
            return jnp.maximum(top, rmax(pair * rowscale[m], 0))

        if last:
            for begin, end in ((0, 4), (4, NZ - 1)):
                rows = (end - begin) * BLOCK
                others = dot(block[begin:end].reshape(rows, width), mine, ((1,), (1,)))
                for m in range(begin, end):
                    top = meet(m, others[(m - begin) * BLOCK : (m - begin + 1) * BLOCK], top)
        else:

            def earlier_block(m, top):
                return meet(m, dot(block[m], mine, ((1,), (1,))), top)

            top = lax.fori_loop(0, n, earlier_block, top)
        best[pl.ds(n, 1), :] = top * scale

        cross = dot(cents[...], mine, ((1,), (1,)))
        member = (fiota((table, BLOCK), 0) + 1.0) == tag
        similar = rsum(jnp.where(member, cross * qcol[...], 0.0), 0) * scale
        simil[pl.ds(n, 1), :] = similar
        tot[0] += one_if(member)
        tot[1] += jnp.where(member, similar, 0.0)
        tot[2] += jnp.where(member, similar * similar, 0.0)

    relay_tags(0, NJ - 1)
    relay(0, NJ - 1, 0)
    load_cents.wait()
    squares = jnp.zeros((table, 128), F32)
    for c in range(width // 128):
        part = cents[:, c * 128 : (c + 1) * 128].astype(F32)
        squares += part * part
    qcol[...] = lax.rsqrt(rsum(squares, 1) + 1.0)


    def main_step(i, carry):
        for n in (2 * i + 1, 2 * i + 2):
            relay_tags(n, NJ)
            relay(n, NJ, n)
        for n in (2 * i + 5, 2 * i + 6):

            @pl.when(n < NZ)
            def _():
                send_docs(n)

        @pl.when(i > 0)
        def _():
            owner_block(2 * i - 1)

        owner_block(2 * i)
        return carry

    lax.fori_loop(0, (NZ - 2) // 2, main_step, 0)
    relay_tags(NZ - 1, NJ)
    relay(NZ - 1, NJ // 2, NZ - 1, 0, NJ // 2)
    owner_block(NZ - 3)
    relay(NZ - 1, NJ // 2, NZ, NJ // 2, NJ // 2)
    owner_block(NZ - 2)
    owner_block(NZ - 1, last=True)

    counts = rsum(tot[0], 1)
    sums = rsum(tot[1], 1)
    squares = rsum(tot[2], 1)
    pos = iota((table, 128), 1)
    stacked = jnp.where(pos == 0, counts, jnp.where(pos == 1, sums, jnp.where(pos == 2, squares, 0.0)))
    stats_ref[...] = stacked.T[:3]
    floor = jnp.maximum(counts, 1.0)
    mean = sums / floor
    spread = jnp.sqrt(jnp.maximum(squares / floor - mean * mean, 0.0) + 1.0 / width)

    def scores(n, carry):
        tag = tags[pl.ds(n, 1), :]
        member = (fiota((table, BLOCK), 0) + 1.0) == tag
        mean_at = rsum(jnp.where(member, mean, 0.0), 0)
        spread_at = rsum(jnp.where(member, spread, 0.0), 0)
        gap = (mean_at - simil[pl.ds(n, 1), :]) / jnp.where(tag > 0.0, spread_at, 1.0)
        score[0, pl.ds(n, 1), :] = jnp.where(tag > 0.0, gap, 0.0)
        rows = rmax((rowbest[n] * rowscale[n]).T, 0)
        score[1, pl.ds(n, 1), :] = math.sqrt(width) * jnp.maximum(best[pl.ds(n, 1), :], rows)
        return carry

    lax.fori_loop(0, NZ, scores, 0)
    for dy in range(1, NY):
        y_send(NY - dy, score, score_in.at[dy], score_send, score_recv).start()
    score_in[0] = score[...]

    arrived(score_in.at[pl.ds(1, NY - 1)], score_recv)
    lanes = iota((GROUPS, 128), 1)
    mine = lax.rem(lanes, ROWS) // CAP == lax.rem(iota((GROUPS, 128), 0), NJ)
    from_lane, to_lane = iota((128, 128), 0), iota((128, 128), 1)
    laid = jnp.zeros((GROUPS, 128), F32)
    for s in range(2):
        held = jnp.zeros((NZ, 128), F32)
        for dy in range(NY):
            held = jnp.where(iota((NZ, 128), 1) // ROWS == dy, score_in[dy, s], held)
        held = jnp.broadcast_to(held[:, None, :], (NZ, NJ, 128)).reshape(GROUPS, 128)
        move = one_if(to_lane == (from_lane // ROWS) * (2 * CAP) + s * CAP + lax.rem(from_lane, CAP))
        laid += dot(jnp.where(mine, held, 0.0), move, precision=HIGHEST)
    for g in range(GROUPS):
        reply[g] = laid[g : g + 1, :]

    for n in reversed(range(NZ)):
        send_group(reply, reply_in, (reply_send, reply_recv), n, sign=-1)
    reply_in[0] = reply[0]

    for n, dz in enumerate(STEPS):
        arrived(inbox.at[pl.ds(0, NJ - 1 if dz == 0 else NJ)], doc_send.at[n])
        arrived(fwd.at[n], fwd_send.at[n])
    arrived(tag_out.at[pl.ds(0, GROUPS - 1)], tag_send)
    for dy in range(1, NY):
        arrived(own_in.at[dy], own_send)
    arrived(score_in.at[pl.ds(1, NY - 1)], score_send)
    arrived(reply.at[pl.ds(0, GROUPS - 1)], reply_send)
    arrived(reply_in.at[pl.ds(0, GROUPS - 1)], reply_recv)


def unpack(reply_ref, assign, place, stats_ref, proto_ref, red_ref, totals_ref):
    count = assign.shape[1]
    home = jnp.concatenate(
        [reply_ref[...].reshape(GROUPS, 128), jnp.zeros((128 - GROUPS, 128), F32)], axis=0
    ).T
    picked = dot(home[: NY * 2 * CAP, :GROUPS], assign[...], precision=HIGHEST)
    at = fiota((NY * 2 * CAP, count), 0)
    proto_ref[...] = rsum(jnp.where(at == place[...], picked, 0.0), 0)
    red_ref[...] = rsum(jnp.where(at == place[...] + CAP, picked, 0.0), 0)
    totals_ref[...] = stats_ref[...]


def local(documents, assigned, centroids, owner_slot):
    count, width = documents.shape
    table = centroids.shape[0]
    wide = width + width // 4
    dma = pltpu.SemaphoreType.DMA
    outs = (
        jax.ShapeDtypeStruct((1, count), F32),
        jax.ShapeDtypeStruct((1, count), F32),
        jax.ShapeDtypeStruct((3, table), F32),
    )
    vmem = pl.BlockSpec(memory_space=pltpu.VMEM)
    parts = pl.pallas_call(
        kernel,
        out_shape=(
            jax.ShapeDtypeStruct((GROUPS, 1, 128), F32),
            jax.ShapeDtypeStruct((GROUPS, count), F32),
            jax.ShapeDtypeStruct((1, count), F32),
            jax.ShapeDtypeStruct((3, table), F32),
        ),
        in_specs=[pl.BlockSpec(memory_space=pl.ANY)] * 4,
        out_specs=(vmem,) * 4,
        scratch_shapes=[
            pltpu.VMEM((1, count), jnp.int32),
            pltpu.VMEM((owner_slot.shape[0] // 128, 128), jnp.int32),
            pltpu.VMEM((count, width), BF16),
            pltpu.VMEM((table, width), BF16),
            pltpu.VMEM((GROUPS, MAIN, wide), BF16),
            pltpu.VMEM((GROUPS, MAIN, wide), BF16),
            pltpu.VMEM((NZ, BLOCK - ROWS, width), BF16),
            pltpu.VMEM((NZ, BLOCK, width), BF16),
            pltpu.VMEM((GROUPS, 1, 256), F32),
            pltpu.VMEM((GROUPS, 1, 256), F32),
            pltpu.VMEM((NZ, 1, 256), F32),
            pltpu.VMEM((NY, NZ, 1, 256), F32),
            pltpu.VMEM((table, 1), F32),
            pltpu.VMEM((NZ, BLOCK), F32),
            pltpu.VMEM((NZ, BLOCK, BLOCK), F32),
            pltpu.VMEM((NZ, BLOCK, BLOCK), F32),
            pltpu.VMEM((NZ, BLOCK), F32),
            pltpu.VMEM((NZ, BLOCK), F32),
            pltpu.VMEM((NZ, BLOCK, BLOCK), F32),
            pltpu.VMEM((3, table, BLOCK), F32),
            pltpu.VMEM((2, NZ, BLOCK), F32),
            pltpu.VMEM((NY, 2, NZ, BLOCK), F32),
            pltpu.VMEM((GROUPS, 1, 128), F32),
            pltpu.SemaphoreType.REGULAR((NZ // 2, 2)),
            dma((4,)),
            dma((NZ,)), dma((NZ + 1,)),
            dma, dma((NZ,)),
            dma, dma((NZ,)),
            dma((NZ,)), dma((NZ,)),
            dma, dma,
            dma, dma,
        ],
        compiler_params=pltpu.CompilerParams(
            collective_id=0, has_side_effects=True, vmem_limit_bytes=56 * 1024 * 1024
        ),
        name="route_and_score",
    )(assigned.reshape(1, count), owner_slot.reshape(-1, 128), documents, centroids)
    proto, red, stats = pl.pallas_call(
        unpack,
        out_shape=outs,
        in_specs=[vmem] * 4,
        out_specs=(vmem,) * 3,
        name="unpack",
    )(*parts)
    return proto.reshape(count), red.reshape(count), stats


def solution(mesh):
    split = Mesh(mesh.devices.reshape(NX, NZ, NK, NY), AXES)
    placed = (P(AXES, None), P(AXES), P(AXES, None), P())
    return jax.shard_map(
        local,
        mesh=split,
        in_specs=placed,
        out_specs=(P(AXES), P(AXES), P(None, AXES)),
        check_vma=False,
    )
```

time: 119 us -> 108 us (0.908)
  local copies, waits for them, and re-layouts: 8.3 us -> 0 us
  Pallas kernels: 109 us -> 107 us
    gather x1 -> x0, local copies, waits for them, and re-layouts: 4.27 us -> none  [local(): slot = owner_slot[assigned].reshape(1, count)]
    unnamed x5 -> x0, local copies, waits for them, and re-layouts: 4.03 us -> none
    pallas_call x1 -> x2, Pallas kernels: 109 us -> 107 us  [the longest x1 105 us: local(): pl.pallas_call(kernel, out_shape=(jax.ShapeDtypeStruct((GROUPS, 1, 128),...]
where the time goes in v2:
time: 108 us; the launch traced here: 107 us
  Pallas kernels  107 us (99%)
    pallas_call x1, Pallas kernels, local(): pl.pallas_call(kernel, out_shape=(jax.ShapeDtypeStruct((GROUPS, 1, 128),...  105 us

profile of v2, /device:TPU:1, one launch (start us, length us, event | category | flops | bytes accessed | tf_op | source)
XLA Modules:
  0.0 107.4 jit_solution(16838946398925411804)
XLA Ops:
  0.6 105.0 %route_and_score.1 = (f32[64,1,128]{2,1,0:T(1,128)}, f32[64,512]{1,0:T(8,128)}, f32[1,512]{1,0:T(1,128)}, f32[3,384]{1,0:T(4,128)}) custom-call(s32[1,512]{1,0:T(1,128)} %bitcast.5, s32[768,128]{1,0:T(8,128)} %bitcast.4, bf16[512,2048]{1,0:T(8,128)(2,1)} %docs_hbm.1, bf16[384,2048]{1,0:T(8,128)(2,1)} %cents_hbm.1), custom_call_target="tpu_custom_call" | custom-call | tf_op jit(solution)/shard_map/route_and_score/pallas_call | solution.py:461
  105.6 1.8 %unpack.1 = (f32[1,512]{1,0:T(1,128)}, f32[1,512]{1,0:T(1,128)}, f32[3,384]{1,0:T(4,128)}) custom-call(f32[64,1,128]{2,1,0:T(1,128)} %get-tuple-element.10.reply_ref, f32[64,512]{1,0:T(8,128)} %get-tuple-element.11.assign, f32[1,512]{1,0:T(1,128)} %get-tuple-element.12.place, f32[3,384]{1,0:T(4,128)} %get-tuple-element.13.stats_ref), custom_call_target="tpu_custom_call" | custom-call | tf_op jit(solution)/shard_map/unpack/pallas_call | solution.py:509

commit v3 on v2

--- a/solution.py
+++ b/solution.py
@@ -20,6 +20,7 @@
 MAIN, SPILL, CAP = 8, 2, 4
 STEPS = tuple((n + 1) // 2 if n % 2 else -(n // 2) % NZ for n in range(NZ))
 ROWS = NJ * CAP
+PLANE_FIRST, PLANE_THEN = (1, 2, 3), (4, 0, 5, 6, 7)
 BLOCK = NY * ROWS
 
 
@@ -49,12 +50,12 @@
 
 def kernel(
     assigned_hbm, slots_hbm, docs_hbm, cents_hbm,
-    reply_in, assign, place, stats_ref,
-    assigned, slots, docs, cents, out, inbox, fwd, block,
+    reply_in, group_ref, place, stats_ref,
+    assigned, slots, docs, cents, out, mid, inbox, fwd, block,
     tag_out, tag_in, own_out, own_in,
     qcol, tags, rowscale, rowtag, simil, best, rowbest, tot,
     score, score_in, reply,
-    ring, load_sem, doc_send, doc_recv, tag_send, tag_recv, own_send, own_recv,
+    ring, load_sem, doc_send, hop_send, mid_recv, doc_recv, tag_send, tag_recv, own_send, own_recv,
     fwd_send, fwd_recv, score_send, score_recv, reply_send, reply_recv,
 ):
     x, z, k, y = (lax.axis_index(a) for a in AXES)
@@ -145,7 +146,7 @@
     is_main = rank < float(MAIN)
     main_at = jnp.where(is_main, group * MAIN + rank, -1.0)
     spill_at = jnp.where(is_main, -8.0, group * MAIN + (rank - MAIN) * 4.0)
-    assign[...] = at_group
+    group_ref[...] = group
     place[...] = col * (2.0 * CAP) + rank_owner
 
     value = col * float(ROWS) + turn * CAP + rank_owner + 1.0
@@ -197,23 +198,40 @@
 
         lax.fori_loop(max(first, 1 if n == 0 else 0), last, body, 0)
 
-    def send_docs(n):
-        odd = lax.rem(n, 2)
-        dz = lax.rem(odd * ((n + 1) // 2) + (1 - odd) * (NZ - n // 2), NZ)
+    def plane_send(n):
+        ref_in, sems = (mid, (hop_send, mid_recv.at[n])) if n else (inbox, (doc_send.at[0], doc_recv.at[0]))
 
         def body(t, carry):
-            px, pz, pk = peer(dz, t)
+            px, pz, pk = peer(0, t)
             pltpu.make_async_remote_copy(
                 src_ref=out.at[n * NJ + t],
-                dst_ref=inbox.at[n * NJ + t],
-                send_sem=doc_send.at[n],
-                recv_sem=doc_recv.at[n + (n // (NZ - 1)) * (t // (NJ // 2))],
+                dst_ref=ref_in.at[n * NJ + t],
+                send_sem=sems[0],
+                recv_sem=sems[1],
                 device_id=(px, pz, pk, y),
                 device_id_type=MESH,
             ).start()
             return carry
 
-        lax.fori_loop(1 if isinstance(n, int) and n == 0 else 0, NJ, body, 0)
+        lax.fori_loop(1, NJ, body, 0)
+
+    def z_send(n, ref_out, first, many):
+        odd = lax.rem(n, 2)
+        dz = lax.rem(odd * ((n + 1) // 2) + (1 - odd) * (NZ - n // 2), NZ)
+        rows = pl.ds(n * NJ + first, many)
+        pltpu.make_async_remote_copy(
+            src_ref=ref_out.at[rows],
+            dst_ref=inbox.at[rows],
+            send_sem=doc_send.at[n],
+            recv_sem=doc_recv.at[n + (n // (NZ - 1)) * (first // (NJ // 2))],
+            device_id=(x, lax.rem(z + dz, NZ), k, y),
+            device_id_type=MESH,
+        ).start()
+
+    def z_forward(n):
+        arrived(mid.at[pl.ds(0, NJ - 1)], mid_recv.at[n])
+        z_send(n, mid, 1, NJ // 2 - 1)
+        z_send(n, mid, NJ // 2, NJ // 2)
 
     def send_tags(n):
         send_group(tag_out, tag_in, (tag_send, tag_recv.at[n]), n)
@@ -232,27 +250,32 @@
     pl.semaphore_wait(barrier, NJ - 1 + NY - 1 + 2)
     ring_signal(0)
     send_tags(0)
-    send_docs(0)
+    for n in PLANE_FIRST:
+        plane_send(n)
     ring_wait(0)
     ring_signal(1)
     for n in (1, 2):
         send_tags(n)
-    for n in (1, 2):
-        send_docs(n)
+        z_send(n, out, 0, 1)
     inbox[0] = out[0]
+    pack(1)
     ring_wait(1)
     ring_signal(2)
     for n in (3, 4):
         send_tags(n)
-    send_docs(3)
-    pack(1)
-    send_docs(4)
+        z_send(n, out, 0, 1)
+    for n in PLANE_THEN:
+        plane_send(n)
     ring_wait(2)
     ring_signal(3)
     for n in (5, 6):
         send_tags(n)
+        z_send(n, out, 0, 1)
     ring_wait(3)
     send_tags(7)
+    z_send(7, out, 0, 1)
+    for n in (1, 2, 3, 4):
+        z_forward(n)
 
     tot[...] = jnp.zeros_like(tot)
     best[...] = jnp.zeros_like(best)
@@ -362,7 +385,7 @@
 
             @pl.when(n < NZ)
             def _():
-                send_docs(n)
+                z_forward(n)
 
         @pl.when(i > 0)
         def _():
@@ -428,6 +451,7 @@
         arrived(inbox.at[pl.ds(0, NJ - 1 if dz == 0 else NJ)], doc_send.at[n])
         arrived(fwd.at[n], fwd_send.at[n])
     arrived(tag_out.at[pl.ds(0, GROUPS - 1)], tag_send)
+    arrived(inbox.at[pl.ds(0, (NZ - 1) * (NJ - 1))], hop_send)
     for dy in range(1, NY):
         arrived(own_in.at[dy], own_send)
     arrived(score_in.at[pl.ds(1, NY - 1)], score_send)
@@ -435,12 +459,13 @@
     arrived(reply_in.at[pl.ds(0, GROUPS - 1)], reply_recv)
 
 
-def unpack(reply_ref, assign, place, stats_ref, proto_ref, red_ref, totals_ref):
-    count = assign.shape[1]
+def unpack(reply_ref, group_ref, place, stats_ref, proto_ref, red_ref, totals_ref):
+    count = group_ref.shape[1]
+    assign = one_if(fiota((GROUPS, count), 0) == group_ref[...])
     home = jnp.concatenate(
         [reply_ref[...].reshape(GROUPS, 128), jnp.zeros((128 - GROUPS, 128), F32)], axis=0
     ).T
-    picked = dot(home[: NY * 2 * CAP, :GROUPS], assign[...], precision=HIGHEST)
+    picked = dot(home[: NY * 2 * CAP, :GROUPS], assign, precision=HIGHEST)
     at = fiota((NY * 2 * CAP, count), 0)
     proto_ref[...] = rsum(jnp.where(at == place[...], picked, 0.0), 0)
     red_ref[...] = rsum(jnp.where(at == place[...] + CAP, picked, 0.0), 0)
@@ -462,7 +487,7 @@
         kernel,
         out_shape=(
             jax.ShapeDtypeStruct((GROUPS, 1, 128), F32),
-            jax.ShapeDtypeStruct((GROUPS, count), F32),
+            jax.ShapeDtypeStruct((1, count), F32),
             jax.ShapeDtypeStruct((1, count), F32),
             jax.ShapeDtypeStruct((3, table), F32),
         ),
@@ -473,6 +498,7 @@
             pltpu.VMEM((owner_slot.shape[0] // 128, 128), jnp.int32),
             pltpu.VMEM((count, width), BF16),
             pltpu.VMEM((table, width), BF16),
+            pltpu.VMEM((GROUPS, MAIN, wide), BF16),
             pltpu.VMEM((GROUPS, MAIN, wide), BF16),
             pltpu.VMEM((GROUPS, MAIN, wide), BF16),
             pltpu.VMEM((NZ, BLOCK - ROWS, width), BF16),
@@ -494,7 +520,7 @@
             pltpu.VMEM((GROUPS, 1, 128), F32),
             pltpu.SemaphoreType.REGULAR((NZ // 2, 2)),
             dma((4,)),
-            dma((NZ,)), dma((NZ + 1,)),
+            dma((NZ,)), dma, dma((NZ,)), dma((NZ + 1,)),
             dma, dma((NZ,)),
             dma, dma((NZ,)),
             dma((NZ,)), dma((NZ,)),

time: 108 us -> 103 us (0.954)
  Pallas kernels: 107 us -> 102 us
    pallas_call x1, Pallas kernels: 105 us -> 101 us  [local(): pl.pallas_call(kernel, out_shape=(jax.ShapeDtypeStruct((GROUPS, 1, 128),...]
where the time goes in v3:
time: 103 us
  Pallas kernels  102 us (99%)
    pallas_call x1, Pallas kernels, local(): pl.pallas_call(kernel, out_shape=(jax.ShapeDtypeStruct((GROUPS, 1, 128),...  101 us

profile of v3, /device:TPU:1, one launch (start us, length us, event | category | flops | bytes accessed | tf_op | source)
XLA Modules:
  0.0 103.0 jit_solution(9275244739195292926)
XLA Ops:
  0.6 100.7 %route_and_score.1 = (f32[64,1,128]{2,1,0:T(1,128)}, f32[1,512]{1,0:T(1,128)}, f32[1,512]{1,0:T(1,128)}, f32[3,384]{1,0:T(4,128)}) custom-call(s32[1,512]{1,0:T(1,128)} %bitcast.5, s32[768,128]{1,0:T(8,128)} %bitcast.4, bf16[512,2048]{1,0:T(8,128)(2,1)} %docs_hbm.1, bf16[384,2048]{1,0:T(8,128)(2,1)} %cents_hbm.1), custom_call_target="tpu_custom_call" | custom-call | tf_op jit(solution)/shard_map/route_and_score/pallas_call | solution.py:486
  101.4 1.6 %unpack.1 = (f32[1,512]{1,0:T(1,128)}, f32[1,512]{1,0:T(1,128)}, f32[3,384]{1,0:T(4,128)}) custom-call(f32[64,1,128]{2,1,0:T(1,128)} %get-tuple-element.10.reply_ref, f32[1,512]{1,0:T(1,128)} %get-tuple-element.11.group_ref, f32[1,512]{1,0:T(1,128)} %get-tuple-element.12.place, f32[3,384]{1,0:T(4,128)} %get-tuple-element.13.stats_ref), custom_call_target="tpu_custom_call" | custom-call | tf_op jit(solution)/shard_map/unpack/pallas_call | solution.py:535

commit v4 on v3

--- a/solution.py
+++ b/solution.py
@@ -367,8 +367,6 @@
         tot[1] += jnp.where(member, similar, 0.0)
         tot[2] += jnp.where(member, similar * similar, 0.0)
 
-    relay_tags(0, NJ - 1)
-    relay(0, NJ - 1, 0)
     load_cents.wait()
     squares = jnp.zeros((table, 128), F32)
     for c in range(width // 128):
@@ -378,27 +376,34 @@
 
 
     def main_step(i, carry):
-        for n in (2 * i + 1, 2 * i + 2):
-            relay_tags(n, NJ)
-            relay(n, NJ, n)
-        for n in (2 * i + 5, 2 * i + 6):
-
-            @pl.when(n < NZ)
-            def _():
+        relay_tags(2 * i + 1, NJ)
+        relay(2 * i + 1, NJ, 2 * i + 1)
+
+        @pl.when(i == 0)
+        def _():
+            for n in (5, 6, 7):
                 z_forward(n)
+
+        relay_tags(2 * i + 2, NJ)
+        relay(2 * i + 2, NJ, 2 * i + 2)
+        @pl.when(i == 0)
+        def _():
+            relay_tags(0, NJ - 1)
+            relay(0, NJ - 1, 0)
 
         @pl.when(i > 0)
         def _():
+            owner_block(2 * i - 2)
             owner_block(2 * i - 1)
 
-        owner_block(2 * i)
         return carry
 
     lax.fori_loop(0, (NZ - 2) // 2, main_step, 0)
+    owner_block(NZ - 4)
     relay_tags(NZ - 1, NJ)
     relay(NZ - 1, NJ // 2, NZ - 1, 0, NJ // 2)
+    relay(NZ - 1, NJ // 2, NZ, NJ // 2, NJ // 2)
     owner_block(NZ - 3)
-    relay(NZ - 1, NJ // 2, NZ, NJ // 2, NJ // 2)
     owner_block(NZ - 2)
     owner_block(NZ - 1, last=True)
 

time: 103 us -> 102 us (level)
  no operation moved by 1% of the time
where the time goes in v4:
time: 102 us
  Pallas kernels  102 us (100%)
    pallas_call x1, Pallas kernels, local(): pl.pallas_call(kernel, out_shape=(jax.ShapeDtypeStruct((GROUPS, 1, 128),...  99.9 us

profile of v4, /device:TPU:1, one launch (start us, length us, event | category | flops | bytes accessed | tf_op | source)
XLA Modules:
  0.0 102.2 jit_solution(14075272444492068636)
XLA Ops:
  0.6 99.9 %route_and_score.1 = (f32[64,1,128]{2,1,0:T(1,128)}, f32[1,512]{1,0:T(1,128)}, f32[1,512]{1,0:T(1,128)}, f32[3,384]{1,0:T(4,128)}) custom-call(s32[1,512]{1,0:T(1,128)} %bitcast.5, s32[768,128]{1,0:T(8,128)} %bitcast.4, bf16[512,2048]{1,0:T(8,128)(2,1)} %docs_hbm.1, bf16[384,2048]{1,0:T(8,128)(2,1)} %cents_hbm.1), custom_call_target="tpu_custom_call" | custom-call | tf_op jit(solution)/shard_map/route_and_score/pallas_call | solution.py:491
  100.5 1.6 %unpack.1 = (f32[1,512]{1,0:T(1,128)}, f32[1,512]{1,0:T(1,128)}, f32[3,384]{1,0:T(4,128)}) custom-call(f32[64,1,128]{2,1,0:T(1,128)} %get-tuple-element.10.reply_ref, f32[1,512]{1,0:T(1,128)} %get-tuple-element.11.group_ref, f32[1,512]{1,0:T(1,128)} %get-tuple-element.12.place, f32[3,384]{1,0:T(4,128)} %get-tuple-element.13.stats_ref), custom_call_target="tpu_custom_call" | custom-call | tf_op jit(solution)/shard_map/unpack/pallas_call | solution.py:540

commit v5 on v4

--- a/solution.py
+++ b/solution.py
@@ -309,7 +309,7 @@
             for dy in range(1, NY):
                 at_row = (dy - 1) * ROWS + first * CAP
                 fwd[n, at_row : at_row + tall, cols] = rows[dy * tall : (dy + 1) * tall]
-        for dy in range(1, NY):
+        for dy in (2, 1, 3):
             y_send(
                 dy,
                 fwd.at[n, pl.ds((dy - 1) * ROWS + first * CAP, tall)],
@@ -410,9 +410,6 @@
     counts = rsum(tot[0], 1)
     sums = rsum(tot[1], 1)
     squares = rsum(tot[2], 1)
-    pos = iota((table, 128), 1)
-    stacked = jnp.where(pos == 0, counts, jnp.where(pos == 1, sums, jnp.where(pos == 2, squares, 0.0)))
-    stats_ref[...] = stacked.T[:3]
     floor = jnp.maximum(counts, 1.0)
     mean = sums / floor
     spread = jnp.sqrt(jnp.maximum(squares / floor - mean * mean, 0.0) + 1.0 / width)
@@ -432,6 +429,9 @@
     for dy in range(1, NY):
         y_send(NY - dy, score, score_in.at[dy], score_send, score_recv).start()
     score_in[0] = score[...]
+    pos = iota((table, 128), 1)
+    stacked = jnp.where(pos == 0, counts, jnp.where(pos == 1, sums, jnp.where(pos == 2, squares, 0.0)))
+    stats_ref[...] = stacked.T[:3]
 
     arrived(score_in.at[pl.ds(1, NY - 1)], score_recv)
     lanes = iota((GROUPS, 128), 1)

time: 102 us -> 102 us (level)
  no operation moved by 1% of the time
where the time goes in v5:
time: 102 us
  Pallas kernels  102 us (100%)
    pallas_call x1, Pallas kernels, local(): pl.pallas_call(kernel, out_shape=(jax.ShapeDtypeStruct((GROUPS, 1, 128),...  99.9 us

profile of v5, /device:TPU:1, one launch (start us, length us, event | category | flops | bytes accessed | tf_op | source)
XLA Modules:
  0.0 102.1 jit_solution(9098690508250903442)
XLA Ops:
  0.6 99.9 %route_and_score.1 = (f32[64,1,128]{2,1,0:T(1,128)}, f32[1,512]{1,0:T(1,128)}, f32[1,512]{1,0:T(1,128)}, f32[3,384]{1,0:T(4,128)}) custom-call(s32[1,512]{1,0:T(1,128)} %bitcast.5, s32[768,128]{1,0:T(8,128)} %bitcast.4, bf16[512,2048]{1,0:T(8,128)(2,1)} %docs_hbm.1, bf16[384,2048]{1,0:T(8,128)(2,1)} %cents_hbm.1), custom_call_target="tpu_custom_call" | custom-call | tf_op jit(solution)/shard_map/route_and_score/pallas_call | solution.py:491
  100.5 1.6 %unpack.1 = (f32[1,512]{1,0:T(1,128)}, f32[1,512]{1,0:T(1,128)}, f32[3,384]{1,0:T(4,128)}) custom-call(f32[64,1,128]{2,1,0:T(1,128)} %get-tuple-element.10.reply_ref, f32[1,512]{1,0:T(1,128)} %get-tuple-element.11.group_ref, f32[1,512]{1,0:T(1,128)} %get-tuple-element.12.place, f32[3,384]{1,0:T(4,128)} %get-tuple-element.13.stats_ref), custom_call_target="tpu_custom_call" | custom-call | tf_op jit(solution)/shard_map/unpack/pallas_call | solution.py:540
